TPU v7x, 32 devices: a whole 2x2x4 slice. The times are simulated.
32 devices in a mesh: dp: 8 (over z, y), seq: 4 (over x, core).
Axes of the slice: x: 2, y: 2, z: 4, core: 2. Of those that a mesh axis runs over, the one named last changes fastest.
Arguments:
- tokens: bfloat16 [16, 1024, 1536], P('dp', 'seq'), may hold values from -6 to 6
- in_proj: bfloat16 [1536, 6448], P(('dp', 'seq')), may hold values from -0.15625 to 0.15625
- conv_weight: bfloat16 [4, 3328], P(None, ('dp', 'seq')), may hold values from -3 to 3
- conv_bias: bfloat16 [3328], P(('dp', 'seq')), may hold values from -0.5 to 0.5
- decay_log: float32 [48], replicated, may hold values from -6 to 0.5
- step_bias: float32 [48], replicated, may hold values from -4.5 to -2
- skip_gain: float32 [48], replicated, may hold values from 0.5 to 1.5
- norm_gain: bfloat16 [1536], P(('dp', 'seq')), may hold values from 0.099609375 to 1.8984375
- gated_gain: bfloat16 [3072], P(('dp', 'seq')), may hold values from 0.099609375 to 1.8984375
- out_proj: bfloat16 [3072, 1536], P(('dp', 'seq')), may hold values from -0.109375 to 0.109375
- cotangent: bfloat16 [16, 1024, 1536], P('dp', 'seq'), may hold values from -6 to 6
Outputs:
- block_out: bfloat16 [16, 1024, 1536], P('dp', 'seq')
- tokens_grad: bfloat16 [16, 1024, 1536], P('dp', 'seq')
- in_proj_grad: float32 [1536, 6448], P(('dp', 'seq'))
- conv_weight_grad: float32 [4, 3328], P(None, ('dp', 'seq'))
- conv_bias_grad: float32 [3328], P(('dp', 'seq'))
- decay_log_grad: float32 [48], replicated
- step_bias_grad: float32 [48], replicated
- skip_gain_grad: float32 [48], replicated
- norm_gain_grad: float32 [1536], P(('dp', 'seq'))
- gated_gain_grad: float32 [3072], P(('dp', 'seq'))
- out_proj_grad: float32 [3072, 1536], P(('dp', 'seq'))
All inputs are finite; a program needn't handle non-finite values.
Results may differ from a plain program's by a relative error of at most 0.0062.
Values may be sent and summed in bfloat16 or wider, within the bound.
A program may use at most 256 MiB of HBM per device.

v0:
```python
import jax
import jax.numpy as jnp
from jax import lax
from jax.sharding import PartitionSpec as P

HEADS = 48
P_SIZE = 64
N = 128
KW = 4
GROUP = 256
DI = 3072
CD = 3328
EPSILON = 1e-05
precise = lax.Precision.HIGHEST


def shifted(shard, axis, by):
    peers = lax.axis_size(axis)
    pairs = [(i, i + by) for i in range(peers) if 0 <= i + by < peers]
    return lax.ppermute(shard, axis, pairs)


def entering_2(shard, axis, combine, identity, reverse):
    peers, mine = (lax.axis_size(axis), lax.axis_index(axis))
    everything = jax.tree.map(lambda part: lax.all_gather(part, axis), shard)
    start = jax.tree.map(
        lambda part, zero: jnp.broadcast_to(jnp.asarray(zero, part.dtype), part.shape),
        shard,
        identity,
    )

    def lap(k, before):
        at = peers - 1 - k if reverse else k
        reached = at > mine if reverse else at < mine
        new = combine(before, jax.tree.map(lambda part: part[at], everything))
        return jax.tree.map(lambda a, b: jnp.where(reached, a, b), new, before)

    return lax.fori_loop(0, peers, lap, start)


def group_step(memory, pieces):
    values, inputs_b, inputs_c, step_sizes, decays = pieces
    running = jnp.cumsum(decays, axis=0)
    blocks = decays.shape[0]
    causal = (jnp.arange(blocks)[:, None] >= jnp.arange(blocks)[None, :])[:, :, None]
    spread = running[:, None, :] - running[None, :, :]
    within = jnp.where(causal, jnp.exp(jnp.where(causal, spread, 0.0)), 0.0)
    scores = jnp.dot(inputs_c, inputs_b.T, precision=precise)
    weights = scores[:, :, None] * within * step_sizes[None, :, :]
    output = jnp.einsum("ijh,jhp->ihp", weights, values, precision=precise)
    output = output + jnp.exp(running)[:, :, None] * jnp.einsum(
        "in,hpn->ihp", inputs_c, memory, precision=precise
    )
    closing = running[-1]
    carried = jnp.exp(closing[None, :] - running) * step_sizes
    memory = memory * jnp.exp(closing)[:, None, None] + jnp.einsum(
        "jh,jhp,jn->hpn", carried, values, inputs_b, precision=precise
    )
    return (memory, output)


def local_mixer(projected, halo_rows, conv_weight, conv_bias, decay_log, step_bias, skip_gain):
    length = projected.shape[0]
    gate_half = projected[:, :DI]
    stream = projected[:, DI : DI + CD]
    raw_step = projected[:, DI + CD :]
    padded = jnp.concatenate([halo_rows, stream], axis=0)
    mixed_conv = conv_bias + jnp.zeros_like(stream)
    for offset in range(KW):
        mixed_conv = mixed_conv + conv_weight[offset] * padded[offset : offset + length]
    active = jax.nn.silu(mixed_conv)
    values = active[:, :DI].reshape(length, HEADS, P_SIZE)
    inputs_b = active[:, DI : DI + N]
    inputs_c = active[:, DI + N :]
    step_sizes = jax.nn.softplus(raw_step + step_bias)
    decays = -jnp.exp(decay_log) * step_sizes
    running = jnp.cumsum(decays, axis=0)
    blocks = length // GROUP
    pieces = tuple(
        (
            item.reshape((blocks, GROUP) + item.shape[1:])
            for item in (values, inputs_b, inputs_c, step_sizes, decays)
        )
    )
    memory = jnp.zeros((HEADS, P_SIZE, N), jnp.float32)
    closing, outputs = lax.scan(group_step, memory, pieces)
    partial_out = outputs.reshape(values.shape) + skip_gain[:, None] * values
    return (gate_half, partial_out, closing, running[-1], running, inputs_c)


def prenorm(inputs, norm_gain):
    inv_scale = lax.rsqrt(jnp.mean(inputs * inputs, axis=-1, keepdims=True) + EPSILON)
    return inputs * inv_scale * norm_gain


def gated_norm(ssd_out, gate_half, gated_gain):
    gated = ssd_out.reshape(ssd_out.shape[0], DI) * jax.nn.silu(gate_half)
    gated_scale = lax.rsqrt(jnp.mean(gated * gated, axis=-1, keepdims=True) + EPSILON)
    return gated * gated_scale * gated_gain


def combine(earlier, later):
    return (earlier[0] * later[1][:, None, None] + later[0], earlier[1] * later[1])


def collect(in_proj, conv_weight, conv_bias, norm_gain, gated_gain, out_proj):
    return (
        lax.all_gather(in_proj, ("dp", "seq"), axis=0, tiled=True),
        lax.all_gather(conv_weight, ("dp", "seq"), axis=1, tiled=True),
        lax.all_gather(conv_bias, ("dp", "seq"), axis=0, tiled=True),
        lax.all_gather(norm_gain, ("dp", "seq"), axis=0, tiled=True),
        lax.all_gather(gated_gain, ("dp", "seq"), axis=0, tiled=True),
        lax.all_gather(out_proj, ("dp", "seq"), axis=0, tiled=True),
    )


def share_out(grad_in, grad_conv, grad_bias, grad_norm, grad_gated, grad_out):
    return (
        lax.psum_scatter(grad_in, ("dp", "seq"), scatter_dimension=0, tiled=True),
        lax.psum_scatter(grad_conv, ("dp", "seq"), scatter_dimension=1, tiled=True),
        lax.psum_scatter(grad_bias, ("dp", "seq"), scatter_dimension=0, tiled=True),
        lax.psum_scatter(grad_norm, ("dp", "seq"), scatter_dimension=0, tiled=True),
        lax.psum_scatter(grad_gated, ("dp", "seq"), scatter_dimension=0, tiled=True),
        lax.psum_scatter(grad_out, ("dp", "seq"), scatter_dimension=0, tiled=True),
    )


def body(
    tokens,
    in_proj,
    conv_weight,
    conv_bias,
    decay_log,
    step_bias,
    skip_gain,
    norm_gain,
    gated_gain,
    out_proj,
    cotangent,
):
    micro_count = tokens.shape[0]
    length = tokens.shape[1]
    edge = length - (KW - 1)
    totals = None
    shares = None
    head_totals = (
        jnp.zeros((HEADS,), jnp.float32),
        jnp.zeros((HEADS,), jnp.float32),
        jnp.zeros((HEADS,), jnp.float32),
    )
    block_rows = []
    grad_rows = []
    for micro_index in range(micro_count):
        gathered = collect(in_proj, conv_weight, conv_bias, norm_gain, gated_gain, out_proj)
        w_in, w_conv, b_conv, g_norm, g_gated, w_out = gathered
        inputs = tokens[micro_index].astype(jnp.float32)
        normed_full, norm_back = jax.vjp(prenorm, inputs, g_norm.astype(jnp.float32))
        normed = normed_full.astype(jnp.bfloat16)
        projected = jnp.dot(normed, w_in, preferred_element_type=jnp.float32)
        tail_rows = projected[edge:, DI : DI + CD]
        halo_rows = shifted(tail_rows, "seq", 1)
        mixer_out, mixer_back = jax.vjp(
            local_mixer,
            projected,
            halo_rows,
            w_conv.astype(jnp.float32),
            b_conv.astype(jnp.float32),
            decay_log,
            step_bias,
            skip_gain,
        )
        gate_half, partial_out, closing, total_log, running, inputs_c = mixer_out
        decay_total = jnp.exp(total_log)
        entering, _ = entering_2(
            (closing, decay_total),
            "seq",
            combine,
            (jnp.zeros_like(closing), jnp.ones_like(decay_total)),
            False,
        )
        growth = jnp.exp(running)
        inherited = jnp.einsum("tn,hpn->thp", inputs_c, entering, precision=precise)
        ssd_out = partial_out + growth[:, :, None] * inherited
        shaped_full, norm_gate_back = jax.vjp(
            gated_norm, ssd_out, gate_half, g_gated.astype(jnp.float32)
        )
        shaped = shaped_full.astype(jnp.bfloat16)
        block_rows.append(
            (inputs + jnp.dot(shaped, w_out, preferred_element_type=jnp.float32)).astype(
                jnp.bfloat16
            )
        )
        gathered = collect(in_proj, conv_weight, conv_bias, norm_gain, gated_gain, out_proj)
        w_in, w_conv, b_conv, g_norm, g_gated, w_out = gathered
        upstream = cotangent[micro_index]
        grad_out = jnp.dot(shaped.T, upstream, preferred_element_type=jnp.float32)
        grad_shaped = jnp.dot(upstream, w_out.T, preferred_element_type=jnp.float32)
        grad_ssd, grad_gate, grad_gated = norm_gate_back(grad_shaped)
        weighted = grad_ssd * growth[:, :, None]
        local_back = jnp.einsum("thp,tn->hpn", weighted, inputs_c, precision=precise)
        grad_c = jnp.einsum("thp,hpn->tn", weighted, entering, precision=precise)
        grad_running = growth * jnp.sum(grad_ssd * inherited, axis=2)
        leaving, _ = entering_2(
            (local_back, decay_total),
            "seq",
            combine,
            (jnp.zeros_like(local_back), jnp.ones_like(decay_total)),
            True,
        )
        grad_total = decay_total * jnp.sum(leaving * entering, axis=(1, 2))
        grad_proj, grad_halo, grad_wconv, grad_bconv, grad_decay, grad_step, grad_skip = mixer_back(
            (grad_gate, grad_ssd, leaving, grad_total, grad_running, grad_c)
        )
        returned = shifted(grad_halo.astype(jnp.bfloat16), "seq", -1).astype(grad_halo.dtype)
        grad_proj = grad_proj.at[edge:, DI : DI + CD].add(returned)
        grad_low = grad_proj.astype(jnp.bfloat16)
        grad_in = jnp.dot(normed.T, grad_low, preferred_element_type=jnp.float32)
        grad_normed = jnp.dot(grad_low, w_in.T, preferred_element_type=jnp.float32)
        grad_inputs, grad_norm = norm_back(grad_normed)
        grad_rows.append((upstream.astype(jnp.float32) + grad_inputs).astype(jnp.bfloat16))
        head_totals = (
            head_totals[0] + grad_decay,
            head_totals[1] + grad_step,
            head_totals[2] + grad_skip,
        )
        current = (grad_in, grad_wconv, grad_bconv, grad_norm, grad_gated, grad_out)
        totals = (
            current if totals is None else tuple((old + new for old, new in zip(totals, current)))
        )
    shares = share_out(totals[0], totals[1], totals[2], totals[3], totals[4], totals[5])
    head_sums = lax.psum((head_totals[0], head_totals[1], head_totals[2]), ("dp", "seq"))
    return (
        jnp.stack(block_rows),
        jnp.stack(grad_rows),
        shares[0],
        shares[1],
        shares[2],
        head_sums[0],
        head_sums[1],
        head_sums[2],
        shares[3],
        shares[4],
        shares[5],
    )


def solution(mesh):
    return jax.shard_map(
        body,
        mesh=mesh,
        in_specs=(
            P("dp", "seq", None),
            P(("dp", "seq"), None),
            P(None, ("dp", "seq")),
            P(("dp", "seq")),
            P(),
            P(),
            P(),
            P(("dp", "seq")),
            P(("dp", "seq")),
            P(("dp", "seq"), None),
            P("dp", "seq", None),
        ),
        out_specs=(
            P("dp", "seq", None),
            P("dp", "seq", None),
            P(("dp", "seq"), None),
            P(None, ("dp", "seq")),
            P(("dp", "seq")),
            P(),
            P(),
            P(),
            P(("dp", "seq")),
            P(("dp", "seq")),
            P(("dp", "seq"), None),
        ),
        check_vma=False,
    )
```

profile of v0, /device:TPU:0, one launch (start us, length us, event | category | flops | bytes accessed | tf_op | source)
XLA Modules:
  0.0 1496.8 jit_solution(15407511150518520505)
XLA Ops:
  11.3 44.2 %all-reduce.40 = (bf16[1536]{0:T(1024)(128)(2,1)S(1)}, bf16[3328]{0:T(1024)(128)(2,1)S(1)}, bf16[3072]{0:T(1024)(128)(2,1)}) all-reduce(bf16[1536]{0:T(1024)(128)(2,1)S(1)} %dynamic-update-slice.5, bf16[3328]{0:T(1024)(128)(2,1)S(1)} %dynamic-update-slice.4, ...), channel_id=1, replica_groups=mesh['dp'=8,'seq'=4] {'dp','seq'}, use_global_device_ids=true, to_apply=%add.33 | all-reduce | flops 7936 | bytes 31744
  55.4 41.8 %all-gather.4 = bf16[32,104,4]{1,2,0:T(4,128)(2,1)S(1)} all-gather(bf16[1,104,4]{1,2,0:T(4,128)(2,1)} %bitcast.376), channel_id=1, replica_groups=mesh['dp'=8,'seq'=4] {'dp','seq'}, dimensions={0}, use_global_device_ids=true | all-gather | bytes 27456 | tf_op jit(solution)/shard_map/all_gather | solution.py:109
  101.7 42.9 %all-gather.14.cloned.1.call-done = bf16[1536,6448]{1,0:T(8,128)(2,1)} async-done(((bf16[48,6448]{1,0:T(8,128)(2,1)}), bf16[1536,6448]{1,0:T(8,128)(2,1)}) %all-gather.14.cloned.1.call-update) | async-done | bytes 19808272 | tf_op jit(solution)/shard_map/all_gather | solution.py:108
  144.6 14.3 fusion.195
  161.1 14.7 fusion.198
  207.0 5.8 copy.365
  214.4 11.9 fusion.57
  252.9 8.3 fusion.152
  302.9 7.5 while.51
  314.6 19.0 %fusion.63 = f32[256,48,64]{0,2,1:T(8,128)} fusion(f32[256,48,64]{0,2,1:T(8,128)S(1)} %fusion.184, f32[256,48,64]{0,2,1:T(8,128)S(1)} %bitcast.329, f32[256,48,64]{0,2,1:T(8,128)} %fusion.159, f32[256,48]{0,1:T(8,128)S(1)} %copy-done.93, f32[256,48]{0,1:T(8,128)S(1)} %copy-done.90, f32[256,256]{1,0:T(8,128)S(1)} %copy-done.66, ...), kind=kOutput, calls=%fused_computation.110 | convolution fusion | flops 2436366336 | bytes 13058240 | tf_op jit(solution)/shard_map/jvp()/while/body/eval_jaxpr/ijh,jhp->ihp/dot_general | solution.py:50
  337.1 5.4 multiply_reduce_fusion.22
  342.6 7.3 while.50
  353.7 19.4 %fusion.65 = f32[256,48,64]{0,2,1:T(8,128)} fusion(f32[256,48,64]{0,2,1:T(8,128)S(1)} %fusion.191, f32[256,48,64]{0,2,1:T(8,128)S(1)} %bitcast.338, f32[256,48,64]{0,2,1:T(8,128)} %fusion.162, f32[256,48]{0,1:T(8,128)S(1)} %copy-done.87, f32[256,48]{0,1:T(8,128)S(1)} %copy-done.84, f32[256,256]{1,0:T(8,128)S(1)} %fusion.208, ...), kind=kOutput, calls=%fused_computation.118 | convolution fusion | flops 2436366336 | bytes 13058240 | tf_op jit(solution)/shard_map/jvp()/while/body/eval_jaxpr/ijh,jhp->ihp/dot_general | solution.py:50
  376.6 5.6 multiply_reduce_fusion.23
  382.2 13.5 multiply_reduce_fusion.13
  395.8 15.6 %multiply_reduce_fusion.15 = (f32[3072]{0:T(1024)}, f32[256,3072]{1,0:T(8,128)}, f32[256,3072]{1,0:T(8,128)}, f32[256,3072]{1,0:T(8,128)}, f32[3072]{0:T(1024)}, /*index=5*/f32[256,3072]{1,0:T(8,128)}) fusion(f32[256,3328]{1,0:T(8,128)S(1)} %copy-done.17, f32[256,3072]{1,0:T(8,128)} %copy.364, f32[256,3072]{1,0:T(8,128)} %get-tuple-element.1374, ...), kind=kLoop, calls=%fused_computation.129 | loop fusion | flops 29878272 | bytes 44081152 | tf_op jit(solution)/shard_map/transpose(jvp())/reduce_sum | solution.py:87
  414.9 5.6 fusion.70
  424.4 6.0 fusion.74
  442.2 13.2 fusion.250
  455.5 26.2 %fusion.21 = (f32[256,48]{0,1:T(8,128)}, f32[256,48]{0,1:T(8,128)}, f32[256,48]{0,1:T(8,128)}, f32[256,256]{1,0:T(8,128)}, f32[256,256]{1,0:T(8,128)}, /*index=5...) fusion(f32[256,48]{0,1:T(8,128)S(1)} %copy-done.88, f32[256,48]{0,1:T(8,128)S(1)} %copy-done.85, ...), kind=kOutput, calls=%fused_computation.39 | convolution fusion | flops 2510086144 | bytes 20480000 | tf_op jit(solution)/shard_map/transpose(jvp())/while/body/eval_jaxpr/ijh,jhp->ihp/dot_general | solution.py:50
  503.6 8.1 fusion.144
  511.7 6.1 fusion.141
  517.8 7.9 fusion.154
  525.7 15.4 %while.53 = (s32[]{:T(128)}, f32[48,64,128]{2,1,0:T(8,128)}, s32[]{:T(128)}, f32[4,48]{1,0:T(4,128)}, f32[4,48,64,128]{3,2,1,0:T(8,128)}, /*index=5*/s32[]{:T(128)}, s32[]{:T(128)}, s32[]{:T(128)}, s32[]{:T(128)}) while((s32[]{:T(128)}, f32[48,64,128]{2,1,0:T(8,128)}, s32[]{:T(128)}, f32[4,48]{1,0:T(4,128)}, ...), condition=%wide.region_31.33_spmd.clone, body=%wide.region_30.32_spmd.clone.sunk | while | flops 1572872 | bytes 4719343 | solution.py:38
  541.1 7.5 fusion.138
  548.7 5.9 multiply_reduce_fusion.10
  554.6 7.3 while.52
  561.9 6.4 multiply_reduce_fusion.11
  568.3 5.7 fusion.135
  576.9 12.5 bitcast_add_fusion.4
  593.2 6.6 fusion.249
  602.4 5.7 convolution_bitcast_fusion
  608.1 13.9 bitcast_add_fusion.5
  625.9 6.9 fusion.248
  636.9 7.1 convolution_bitcast_fusion.1
  649.8 7.2 multiply_reduce_fusion.4
  662.5 5.5 broadcast_multiply_fusion
  668.0 6.0 pad_add_fusion.2
  747.5 12.4 fusion.102
  759.9 13.6 fusion.110
  774.1 12.2 convolution_add_fusion.1
  786.5 19.2 %fusion.100 = f32[1536,6448]{1,0:T(8,128)} fusion(f32[256,6448]{1,0:T(8,128)} %scatter-add.9, f32[256]{0:T(256)S(1)} %copy-done.105, f32[1536]{0:T(1024)S(1)} %copy-done.53, bf16[2,256,1536]{2,1,0:T(8,128)(2,1)} %param.24), kind=kOutput, calls=%fused_computation.180 | convolution fusion | flops 5074137088 | bytes 47094784 | tf_op jit(solution)/shard_map/dot_general | solution.py:217
  805.6 31.2 %convolution_add_fusion = f32[1536,6448]{1,0:T(8,128)} fusion(f32[1536,6448]{1,0:T(8,128)} %fusion.100, f32[256,6448]{1,0:T(8,128)} %scatter-add.6, f32[1536]{0:T(1024)S(1)} %copy-done.53, f32[256]{0:T(256)S(1)} %copy-done.103, bf16[2,256,1536]{2,1,0:T(8,128)(2,1)} %param.24), kind=kOutput, calls=%fused_computation.12 | convolution fusion | flops 5084041216 | bytes 87202816 | tf_op jit(solution)/shard_map/dot_general | solution.py:217
  836.9 6.6 fusion.86
  843.6 6.6 fusion.87
  854.9 46.9 %all-reduce.43.cloned.1.call-done = (f32[4,3328]{1,0:T(4,128)}, f32[3328]{0:T(1024)}, f32[48]{0:T(128)}, f32[48]{0:T(128)}, f32[48]{0:T(128)}, /*index=5*/f32[1536]{0:T(1024)}, f32[3072]{0:T(1024)}) async-done(((f32[4,3328]{1,0:T(4,128)}, f32[3328]{0:T(1024)}, f32[48]{0:T(128)}, f32[48]{0:T(128)}, f32[48]{0:T(128)}, /*index=5*/f32[1536]{0:T(1024)}, f32[3072]{0:T(1024)}), (f32[4,3328]{1,0:T(4,128)}, ...) | async-done | bytes 85584
  907.0 209.6 %reduce-scatter.6.cloned.1.call-done = f32[96,1536]{1,0:T(8,128)} async-done(((f32[3072,1536]{1,0:T(8,128)}), f32[96,1536]{1,0:T(8,128)}) %reduce-scatter.6.cloned.1.call-update) | async-done | bytes 589840 | tf_op jit(solution)/shard_map/reduce_scatter | solution.py:124
  1116.6 369.8 %reduce-scatter.4.cloned.1.call-done = f32[48,6448]{1,0:T(8,128)} async-done(((f32[1536,6448]{1,0:T(8,128)}), f32[48,6448]{1,0:T(8,128)}) %reduce-scatter.4.cloned.1.call-update) | async-done | bytes 1238032 | tf_op jit(solution)/shard_map/reduce_scatter | solution.py:119
  (516 shorter events, 319.6 us)
Async XLA Ops:
  7.2 137.5 %all-gather.14.cloned.1.call-start = ((), (), s32[]{:S(2)}) async-start(), calls=%async_computation.2 | async-start | bytes 20680704 | tf_op jit(solution)/shard_map/all_gather | solution.py:108
  7.9 245.0 %all-gather.16.cloned.1.call-start = ((), (), s32[]{:S(2)}) async-start(), calls=%async_computation.3 | async-start | bytes 9732096 | tf_op jit(solution)/shard_map/all_gather | solution.py:113
  8.7 294.2 %all-gather.20.cloned.1.call-start = ((), (), s32[]{:S(2)}) async-start(), calls=%async_computation.7 | async-start | bytes 7864320 | tf_op jit(solution)/shard_map/all_gather | solution.py:25
  55.4 105.6 %copy-start.52 = (f32[1536]{0:T(1024)}, f32[1536]{0:T(1024)S(1)}, u32[]{:S(2)}) copy-start(f32[1536]{0:T(1024)S(1)} %convert_element_type.76) | copy-start | bytes 18436
  98.7 115.7 %copy-start.70 = (f32[3328]{0:T(1024)}, f32[3328]{0:T(1024)S(1)}, u32[]{:S(2)}) copy-start(f32[3328]{0:T(1024)S(1)} %get-tuple-element.1307) | copy-start | bytes 39940
  100.5 58.4 %copy-start.111 = (f32[256]{0:T(256)}, f32[256]{0:T(256)S(1)}, u32[]{:S(2)}) copy-start(f32[256]{0:T(256)S(1)} %get-tuple-element.1301) | copy-start | bytes 3076
  100.5 58.4 %copy-start.113 = (f32[256]{0:T(256)}, f32[256]{0:T(256)S(1)}, u32[]{:S(2)}) copy-start(f32[256]{0:T(256)S(1)} %get-tuple-element.1302) | copy-start | bytes 3076
  101.7 59.4 %copy-start.104 = (f32[256]{0:T(256)}, f32[256]{0:T(256)S(1)}, u32[]{:S(2)}) copy-start(f32[256]{0:T(256)S(1)} %fusion.224) | copy-start | bytes 3076
  101.7 57.2 %copy-start.102 = (f32[256]{0:T(256)}, f32[256]{0:T(256)S(1)}, u32[]{:S(2)}) copy-start(f32[256]{0:T(256)S(1)} %fusion.222) | copy-start | bytes 3076
  184.9 76.3 %copy-start.43 = (f32[48,2,128]{0,2,1:T(8,128)}, f32[48,2,128]{0,2,1:T(8,128)S(1)}, u32[]{:S(2)}) copy-start(f32[48,2,128]{0,2,1:T(8,128)S(1)} %copy.315) | copy-start | bytes 147460
  186.1 28.3 %collective-permute-start = (f32[3,3328]{1,0:T(4,128)}, f32[3,3328]{1,0:T(4,128)}, u32[]{:S(2)}, u32[]{:S(2)}) collective-permute-start(f32[3,3328]{1,0:T(4,128)} %copy.298), channel_id=1, source_target_pairs={{0,1},{1,2},{2,3},{4,5},{5,6},{6,7},{8,9},{9,10},{10,11},{12,13},{... | collective-permute-start | bytes 119816 | tf_op jit(solution)/shard_map/ppermute | solution.py:20
  190.0 24.4 %collective-permute-start.1 = (f32[3,3328]{1,0:T(4,128)}, f32[3,3328]{1,0:T(4,128)}, u32[]{:S(2)}, u32[]{:S(2)}) collective-permute-start(f32[3,3328]{1,0:T(4,128)} %copy.311), channel_id=1, source_target_pairs={{0,1},{1,2},{2,3},{4,5},{5,6},{6,7},{8,9},{9,10},{10,11},{12,13},{... | collective-permute-start | bytes 119816 | tf_op jit(solution)/shard_map/ppermute | solution.py:20
  237.8 104.7 %all-gather.18.cloned.1.call-start = ((), (), s32[]{:S(2)}) async-start(), calls=%async_computation.6 | async-start | bytes 7864320 | tf_op jit(solution)/shard_map/all_gather | solution.py:25
  239.0 26.7 %copy-start.41 = (f32[48,2,128]{0,2,1:T(8,128)}, f32[48,2,128]{0,2,1:T(8,128)S(1)}, u32[]{:S(2)}) copy-start(f32[48,2,128]{0,2,1:T(8,128)S(1)} %copy.302) | copy-start | bytes 147460
  252.0 273.7 %all-gather.24.cloned.1.call-start = ((), (), s32[]{:S(2)}) async-start(), calls=%async_computation.9 | async-start | bytes 7864320 | tf_op jit(solution)/shard_map/all_gather | solution.py:25
  292.4 162.9 %copy-start.65 = (f32[256,256]{1,0:T(8,128)}, f32[256,256]{1,0:T(8,128)S(1)}, u32[]{:S(2)}) copy-start(f32[256,256]{1,0:T(8,128)S(1)} %fusion.208) | copy-start | bytes 786436
  310.4 23.2 %copy-start.2 = (f32[48,64,128]{2,1,0:T(8,128)}, f32[48,64,128]{2,1,0:T(8,128)S(1)}, u32[]{:S(2)}) copy-start(f32[48,64,128]{2,1,0:T(8,128)S(1)} %get-tuple-element.1188) | copy-start | bytes 4718596
  310.4 23.2 %copy-start.122 = (f32[4,48]{1,0:T(4,128)}, f32[4,48]{1,0:T(4,128)S(1)}, u32[]{:S(2)}) copy-start(f32[4,48]{1,0:T(4,128)S(1)} %get-tuple-element.1722) | copy-start | bytes 2308
  314.6 19.0 %copy-start.33 = (f32[256,48,64]{0,2,1:T(8,128)}, f32[256,48,64]{0,2,1:T(8,128)S(1)}, u32[]{:S(2)}) copy-start(f32[256,48,64]{0,2,1:T(8,128)S(1)} %fusion.184) | copy-start | bytes 9437188
  342.6 53.2 %copy-start.106 = (f32[256]{0:T(256)}, f32[256]{0:T(256)S(1)}, u32[]{:S(2)}) copy-start(f32[256]{0:T(256)S(1)} %fusion.225) | copy-start | bytes 3076
  353.7 19.4 %copy-start.34 = (f32[256,48,64]{0,2,1:T(8,128)}, f32[256,48,64]{0,2,1:T(8,128)S(1)}, u32[]{:S(2)}) copy-start(f32[256,48,64]{0,2,1:T(8,128)S(1)} %fusion.191) | copy-start | bytes 9437188
  382.1 135.7 %copy-start.108 = (f32[256]{0:T(256)}, f32[256]{0:T(256)S(1)}, u32[]{:S(2)}) copy-start(f32[256]{0:T(256)S(1)} %fusion.223) | copy-start | bytes 3076
  382.2 13.6 copy-start.17
  420.6 134.1 %all-gather.22.cloned.1.call-start = ((), (), s32[]{:S(2)}) async-start(), calls=%async_computation.8 | async-start | bytes 7864320 | tf_op jit(solution)/shard_map/all_gather | solution.py:25
  430.4 471.4 %all-reduce.43.cloned.1.call-start = ((), (), s32[]{:S(2)}) async-start(), calls=%async_computation.10 | async-start | bytes 183296
  442.1 13.2 copy-start.10
  442.2 13.2 copy-start.12
  442.2 13.2 copy-start.67
  442.2 13.2 copy-start.80
  442.2 13.3 copy-start.85
  442.2 13.3 copy-start.88
  442.2 13.3 copy-start.91
  442.2 13.3 copy-start.94
  501.5 10.2 copy-start.13
  525.7 15.4 %copy-start.62 = (f32[256,48]{0,1:T(8,128)S(1)}, f32[256,48]{0,1:T(8,128)}, u32[]{:S(2)}) copy-start(f32[256,48]{0,1:T(8,128)} %copy.321) | copy-start | bytes 147460
  632.8 17.0 %copy-start.30 = (f32[256,3328]{1,0:T(8,128)S(1)}, f32[256,3328]{1,0:T(8,128)}, u32[]{:S(2)}) copy-start(f32[256,3328]{1,0:T(8,128)} %get-tuple-element.1418) | copy-start | bytes 10223620
  636.9 11.6 copy-start.56
  636.9 12.9 copy-start.21
  681.0 51.3 %copy-start.31 = (f32[256,3328]{1,0:T(8,128)S(1)}, f32[256,3328]{1,0:T(8,128)}, u32[]{:S(2)}) copy-start(f32[256,3328]{1,0:T(8,128)} %split.20) | copy-start | bytes 10223620
  722.5 20.1 %collective-permute-start.3 = (bf16[3,3328]{1,0:T(4,128)(2,1)}, bf16[3,3328]{1,0:T(4,128)(2,1)S(1)}, u32[]{:S(2)}, u32[]{:S(2)}) collective-permute-start(bf16[3,3328]{1,0:T(4,128)(2,1)} %split.24), channel_id=1, source_target_pairs={{1,0},{2,1},{3,2},{5,4},{6,5},{7,6},{9,8},{10,9},{11,10},{13,12},{... | collective-permute-start | bytes 59912 | tf_op jit(solution)/shard_map/ppermute | solution.py:20
  723.8 20.9 %collective-permute-start.2 = (bf16[3,3328]{1,0:T(4,128)(2,1)}, bf16[3,3328]{1,0:T(4,128)(2,1)}, u32[]{:S(2)}, u32[]{:S(2)}) collective-permute-start(bf16[3,3328]{1,0:T(4,128)(2,1)} %split.25), channel_id=1, source_target_pairs={{1,0},{2,1},{3,2},{5,4},{6,5},{7,6},{9,8},{10,9},{11,10},{13,12},{... | collective-permute-start | bytes 59912 | tf_op jit(solution)/shard_map/ppermute | solution.py:20
  747.4 12.4 copy-start.53
  747.4 12.4 copy-start.103
  747.5 12.4 copy-start.105
  759.8 14.3 copy-start.16
  759.9 14.3 copy-start.107
  774.1 342.5 %reduce-scatter.6.cloned.1.call-start = ((), (), s32[]{:S(2)}) async-start(), calls=%async_computation.5 | async-start | bytes 19464192 | tf_op jit(solution)/shard_map/reduce_scatter | solution.py:124
  786.4 700.0 %reduce-scatter.4.cloned.1.call-start = ((), (), s32[]{:S(2)}) async-start(), calls=%async_computation.4 | async-start | bytes 41361408 | tf_op jit(solution)/shard_map/reduce_scatter | solution.py:119
  (97 other events, 495.2 us)
Sparse Core Ops, SparseCore 0:
  10.9 133.7 all-gather.13
  147.5 79.7 all-gather.15
  237.9 44.7 all-gather.19
  284.7 46.3 all-gather.17
  420.7 44.7 all-gather.23
  466.9 46.3 all-gather.21
  774.2 127.5 all-reduce.42
  908.8 207.7 reduce-scatter.5
  1123.6 362.7 reduce-scatter.3
where the time goes:
time: 1510 us; the launch traced here: 1500 us
  waiting for transfers between devices  671 us (44%)
  matrix products  366 us (24%)
  other arithmetic  179 us (12%)
  local copies, waits for them, and re-layouts  158 us (10%)
  blocking collectives  96.1 us (6%)
  between operations  16 us (1%)
    reduce_scatter x1, waiting for transfers between devices, share_out(): lax.psum_scatter(grad_in, ('dp', 'seq'), scatter_dimension=0, tiled=True)  370 us
    reduce_scatter x1, waiting for transfers between devices, share_out(): lax.psum_scatter(grad_out, ('dp', 'seq'), scatter_dimension=0, tiled=True)  210 us
    dot_general x6, matrix products, group_step(): output = jnp.einsum('ijh,jhp->ihp', weights, values, precision=precise)  104 us
    dot_general x2, matrix products, body(): grad_in = jnp.dot(normed.T, grad_low, preferred_element_type=jnp.float32)  50.4 us
    unnamed x10, waiting for transfers between devices  48.4 us
    unnamed x1, blocking collectives  44.2 us
    all_gather x1, waiting for transfers between devices, collect(): lax.all_gather(in_proj, ('dp', 'seq'), axis=0, tiled=True)  42.9 us
    all_gather x1, blocking collectives, collect(): lax.all_gather(conv_weight, ('dp', 'seq'), axis=1, tiled=True)  41.8 us
  transfers between devices with their start and end apart: 13, of which 4 were waited for; matrix products, arithmetic and copies ran while one was open for 28% of the time, Pallas kernels for 0%

commit v1 on v0

--- a/solution.py
+++ b/solution.py
@@ -12,6 +12,29 @@
 CD = 3328
 EPSILON = 1e-05
 precise = lax.Precision.HIGHEST
+
+
+def _pass_chunk(patch, k_dim):
+    patch = jnp.moveaxis(patch, 0, k_dim)
+    local_part = patch.shape
+    e_now = patch.reshape(
+        *local_part[:k_dim], local_part[k_dim] * local_part[k_dim + 1], *local_part[k_dim + 2 :]
+    )
+    return e_now
+
+
+def draw_chunk(local_x, mesh_name):
+    v1, t1 = (lax.psum(1, mesh_name), lax.axis_index(mesh_name))
+    u1, p_next = (local_x[None], 1)
+    while p_next < v1:
+        xs_all = []
+        for num in [*range(v1)]:
+            xs_all.append((num, num ^ p_next))
+        kept_arr = lax.ppermute(u1, mesh_name, xs_all)
+        heard = t1 & p_next == 0
+        u1 = jnp.concatenate([jnp.where(heard, u1, kept_arr), jnp.where(heard, kept_arr, u1)])
+        p_next *= 2
+    return u1
 
 
 def shifted(shard, axis, by):
@@ -104,8 +127,13 @@
 
 
 def collect(in_proj, conv_weight, conv_bias, norm_gain, gated_gain, out_proj):
+
+    def feed_core(tile_in, xin, on_dim=0):
+        base_arr = _pass_chunk(draw_chunk(tile_in, xin), on_dim)
+        return base_arr
+
     return (
-        lax.all_gather(in_proj, ("dp", "seq"), axis=0, tiled=True),
+        feed_core(in_proj, ("dp", "seq")),
         lax.all_gather(conv_weight, ("dp", "seq"), axis=1, tiled=True),
         lax.all_gather(conv_bias, ("dp", "seq"), axis=0, tiled=True),
         lax.all_gather(norm_gain, ("dp", "seq"), axis=0, tiled=True),

time: 1510 us -> 2120 us (1.40)
  blocking collectives: 96.1 us -> 521 us
  waiting for transfers between devices: 671 us -> 816 us
  other arithmetic: 179 us -> 213 us
    unnamed x1, blocking collectives: 44.2 us -> 471 us
    ppermute x0 -> x5, waiting for transfers between devices: none -> 192 us  [draw_chunk(): kept_arr = lax.ppermute(u1, mesh_name, xs_all)]
    all_gather x1 -> x0, waiting for transfers between devices: 42.9 us -> none  [collect(): lax.all_gather(in_proj, ('dp', 'seq'), axis=0, tiled=True)]
    unnamed x10 -> x9, waiting for transfers between devices: 48.4 us -> 45.3 us
  transfers between devices with their start and end apart: 13 -> 17, of which waited for: 4 -> 7; matrix products, arithmetic and copies ran while one was open for 28% -> 21% of each run, Pallas kernels for 0% -> 0%
where the time goes in v1:
time: 2120 us; the launch traced here: 2110 us
  waiting for transfers between devices  816 us (38%)
  blocking collectives  521 us (25%)
  matrix products  367 us (17%)
  other arithmetic  213 us (10%)
  local copies, waits for them, and re-layouts  160 us (8%)
    unnamed x1, blocking collectives  471 us
    reduce_scatter x1, waiting for transfers between devices, share_out(): lax.psum_scatter(grad_in, ('dp', 'seq'), scatter_dimension=0, tiled=True)  370 us
    reduce_scatter x1, waiting for transfers between devices, share_out(): lax.psum_scatter(grad_out, ('dp', 'seq'), scatter_dimension=0, tiled=True)  210 us
    ppermute x5, waiting for transfers between devices, draw_chunk(): kept_arr = lax.ppermute(u1, mesh_name, xs_all)  192 us
    dot_general x6, matrix products, group_step(): output = jnp.einsum('ijh,jhp->ihp', weights, values, precision=precise)  104 us
    dot_general x2, matrix products, body(): grad_in = jnp.dot(normed.T, grad_low, preferred_element_type=jnp.float32)  50.2 us
    unnamed x9, waiting for transfers between devices  45.3 us
  transfers between devices with their start and end apart: 17, of which 7 were waited for; matrix products, arithmetic and copies ran while one was open for 21% of the time, Pallas kernels for 0%

profile of v1, /device:TPU:0, one launch (start us, length us, event | category | flops | bytes accessed | tf_op | source)
XLA Modules:
  0.0 2111.2 jit_solution(12488806520332102096)
XLA Ops:
  14.9 28.1 %collective-permute-done.1 = bf16[2,48,6448]{2,1,0:T(8,128)(2,1)S(1)} collective-permute-done((bf16[2,48,6448]{2,1,0:T(8,128)(2,1)}, bf16[2,48,6448]{2,1,0:T(8,128)(2,1)S(1)}, u32[]{:S(2)}, u32[]{:S(2)}) %collective-permute-start.1) | collective-permute-done | bytes 1238048 | tf_op jit(solution)/shard_map/ppermute | solution.py:33
  46.5 54.2 %collective-permute-done.2 = bf16[4,48,6448]{2,1,0:T(8,128)(2,1)} collective-permute-done((bf16[4,48,6448]{2,1,0:T(8,128)(2,1)S(1)}, bf16[4,48,6448]{2,1,0:T(8,128)(2,1)}, u32[]{:S(2)}, u32[]{:S(2)}) %collective-permute-start.2) | collective-permute-done | bytes 2476064 | tf_op jit(solution)/shard_map/ppermute | solution.py:33
  108.2 107.5 %collective-permute-done.3 = bf16[8,48,6448]{2,1,0:T(8,128)(2,1)} collective-permute-done((bf16[8,48,6448]{2,1,0:T(8,128)(2,1)}, bf16[8,48,6448]{2,1,0:T(8,128)(2,1)}, u32[]{:S(2)}, u32[]{:S(2)}) %collective-permute-start.3) | collective-permute-done | bytes 4952096 | tf_op jit(solution)/shard_map/ppermute | solution.py:33
  229.9 470.5 %all-reduce.40 = (bf16[1536]{0:T(1024)(128)(2,1)S(1)}, bf16[3328]{0:T(1024)(128)(2,1)S(1)}, bf16[3072]{0:T(1024)(128)(2,1)}) all-reduce(bf16[1536]{0:T(1024)(128)(2,1)S(1)} %dynamic-update-slice.5, bf16[3328]{0:T(1024)(128)(2,1)S(1)} %dynamic-update-slice.4, ...), channel_id=1, replica_groups=mesh['dp'=8,'seq'=4] {'dp','seq'}, use_global_device_ids=true, to_apply=%add.33 | all-reduce | flops 7936 | bytes 31744
  700.4 40.0 %all-gather.4 = bf16[32,104,4]{1,2,0:T(4,128)(2,1)S(1)} all-gather(bf16[1,104,4]{1,2,0:T(4,128)(2,1)S(1)} %bitcast.437), channel_id=1, replica_groups=mesh['dp'=8,'seq'=4] {'dp','seq'}, dimensions={0}, use_global_device_ids=true | all-gather | bytes 27456 | tf_op jit(solution)/shard_map/all_gather | solution.py:137
  742.8 8.5 broadcast_select_fusion.1
  751.3 9.9 pad_maximum_fusion
  761.2 14.8 fusion.167
  778.0 14.7 fusion.164
  822.4 5.8 copy.365
  829.8 11.9 fusion.57
  868.8 8.3 fusion.172
  919.0 7.4 while.51
  930.6 19.0 fusion.63
  958.6 7.3 while.50
  969.7 19.2 fusion.65
  998.0 13.5 multiply_reduce_fusion.13
  1011.6 15.6 multiply_reduce_fusion.15
  1040.5 5.9 fusion.74
  1058.3 13.2 fusion.276
  1071.6 26.1 %fusion.21 = (f32[256,48]{0,1:T(8,128)}, f32[256,48]{0,1:T(8,128)}, f32[256,48]{0,1:T(8,128)}, f32[256,256]{1,0:T(8,128)}, f32[256,256]{1,0:T(8,128)}, /*index=5...) fusion(f32[256,48]{0,1:T(8,128)S(1)} %copy-done.93, f32[256,48]{0,1:T(8,128)S(1)} %copy-done.90, ...), kind=kOutput, calls=%fused_computation.43 | convolution fusion | flops 2510086144 | bytes 20480000 | tf_op jit(solution)/shard_map/transpose(jvp())/while/body/eval_jaxpr/ijh,jhp->ihp/dot_general | solution.py:73
  1119.7 8.0 fusion.156
  1127.7 5.9 fusion.153
  1133.7 7.9 fusion.174
  1141.6 15.4 while.53
  1157.0 7.5 fusion.150
  1164.6 5.9 multiply_reduce_fusion.10
  1170.5 7.3 while.52
  1177.8 6.7 multiply_reduce_fusion.11
  1184.5 5.7 fusion.147
  1193.1 12.5 bitcast_add_fusion.4
  1209.4 6.6 fusion.275
  1218.5 5.7 convolution_bitcast_fusion
  1224.2 13.9 bitcast_add_fusion.5
  1242.0 6.9 fusion.274
  1252.8 7.1 convolution_bitcast_fusion.1
  1265.8 7.2 multiply_reduce_fusion.4
  1284.0 6.0 pad_add_fusion.2
  1361.0 12.4 fusion.110
  1376.2 13.6 fusion.118
  1390.4 12.3 convolution_add_fusion.1
  1402.8 19.1 fusion.108
  1421.9 31.2 %convolution_add_fusion = f32[1536,6448]{1,0:T(8,128)} fusion(f32[1536,6448]{1,0:T(8,128)} %fusion.108, f32[256,6448]{1,0:T(8,128)} %scatter-add.6, f32[256]{0:T(256)S(1)} %copy-done.108, f32[1536]{0:T(1024)S(1)} %copy-done.58, bf16[2,256,1536]{2,1,0:T(8,128)(2,1)} %param.24), kind=kOutput, calls=%fused_computation.12 | convolution fusion | flops 5084041216 | bytes 87202816 | tf_op jit(solution)/shard_map/dot_general | solution.py:245
  1453.1 6.6 fusion.86
  1459.8 6.5 fusion.87
  1471.0 45.1 %all-reduce.43.cloned.1.call-done = (f32[4,3328]{1,0:T(4,128)}, f32[3328]{0:T(1024)}, f32[48]{0:T(128)}, f32[48]{0:T(128)}, f32[48]{0:T(128)}, /*index=5*/f32[1536]{0:T(1024)}, f32[3072]{0:T(1024)}) async-done(((f32[4,3328]{1,0:T(4,128)}, f32[3328]{0:T(1024)}, f32[48]{0:T(128)}, f32[48]{0:T(128)}, f32[48]{0:T(128)}, /*index=5*/f32[1536]{0:T(1024)}, f32[3072]{0:T(1024)}), (f32[4,3328]{1,0:T(4,128)}, ...) | async-done | bytes 85584
  1521.3 209.6 %reduce-scatter.6.cloned.1.call-done = f32[96,1536]{1,0:T(8,128)} async-done(((f32[3072,1536]{1,0:T(8,128)}), f32[96,1536]{1,0:T(8,128)}) %reduce-scatter.6.cloned.1.call-update) | async-done | bytes 589840 | tf_op jit(solution)/shard_map/reduce_scatter | solution.py:152
  1730.9 369.7 %reduce-scatter.4.cloned.1.call-done = f32[48,6448]{1,0:T(8,128)} async-done(((f32[1536,6448]{1,0:T(8,128)}), f32[48,6448]{1,0:T(8,128)}) %reduce-scatter.4.cloned.1.call-update) | async-done | bytes 1238032 | tf_op jit(solution)/shard_map/reduce_scatter | solution.py:147
  (553 shorter events, 367.9 us)
Async XLA Ops:
  7.2 861.6 %all-gather.13.cloned.1.call-start = ((), (), s32[]{:S(2)}) async-start(), calls=%async_computation.2 | async-start | bytes 9732096 | tf_op jit(solution)/shard_map/all_gather | solution.py:141
  7.2 2.5 collective-permute-start
  12.1 30.9 %collective-permute-start.1 = (bf16[2,48,6448]{2,1,0:T(8,128)(2,1)}, bf16[2,48,6448]{2,1,0:T(8,128)(2,1)S(1)}, u32[]{:S(2)}, u32[]{:S(2)}) collective-permute-start(bf16[2,48,6448]{2,1,0:T(8,128)(2,1)} %pad_maximum_fusion.8), channel_id=1, source_target_pairs={{0,2},{1,3},{2,0},{3,1},{4,6},{5,7},{6,4},{7,5},{8,10},{9,11},{10,... | collective-permute-start | bytes 3714056 | tf_op jit(solution)/shard_map/ppermute | solution.py:33
  44.7 56.0 %collective-permute-start.2 = (bf16[4,48,6448]{2,1,0:T(8,128)(2,1)S(1)}, bf16[4,48,6448]{2,1,0:T(8,128)(2,1)}, u32[]{:S(2)}, u32[]{:S(2)}) collective-permute-start(bf16[4,48,6448]{2,1,0:T(8,128)(2,1)S(1)} %pad_maximum_fusion.5), channel_id=1, source_target_pairs={{0,4},{1,5},{2,6},{3,7},{4,0},{5,1},{6,2},{7,3},{8,12},{9,13},{10,... | collective-permute-start | bytes 7428104 | tf_op jit(solution)/shard_map/ppermute | solution.py:33
  106.7 109.1 %collective-permute-start.3 = (bf16[8,48,6448]{2,1,0:T(8,128)(2,1)}, bf16[8,48,6448]{2,1,0:T(8,128)(2,1)}, u32[]{:S(2)}, u32[]{:S(2)}) collective-permute-start(bf16[8,48,6448]{2,1,0:T(8,128)(2,1)} %pad_maximum_fusion.2), channel_id=1, source_target_pairs={{0,8},{1,9},{2,10},{3,11},{4,12},{5,13},{6,14},{7,15},{8,0},{9,1},... | collective-permute-start | bytes 14856200 | tf_op jit(solution)/shard_map/ppermute | solution.py:33
  219.9 480.5 %copy-start.128 = (bf16[4,104]{1,0:T(4,128)(2,1)S(1)}, bf16[4,104]{1,0:T(4,128)(2,1)}, u32[]{:S(2)}) copy-start(bf16[4,104]{1,0:T(4,128)(2,1)} %param.26) | copy-start | bytes 2500
  220.0 521.9 %copy-start.30 = (bf16[2,256,1536]{2,1,0:T(8,128)(2,1)S(1)}, bf16[2,256,1536]{2,1,0:T(8,128)(2,1)}, u32[]{:S(2)}) copy-start(bf16[2,256,1536]{2,1,0:T(8,128)(2,1)} %param.24) | copy-start | bytes 4718596
  220.0 522.3 %copy-start.135 = (f32[48]{0:T(128)S(1)}, f32[48]{0:T(128)}, u32[]{:S(2)}) copy-start(f32[48]{0:T(128)} %param.28) | copy-start | bytes 580
  226.8 516.1 %collective-permute-start.4 = (bf16[16,48,6448]{2,1,0:T(8,128)(2,1)}, bf16[16,48,6448]{2,1,0:T(8,128)(2,1)}, u32[]{:S(2)}, u32[]{:S(2)}) collective-permute-start(bf16[16,48,6448]{2,1,0:T(8,128)(2,1)} %pad_maximum_fusion.1), channel_id=1, source_target_pairs={{0,16},{1,17},{2,18},{3,19},{4,20},{5,21},{6,22},{7,23},{8,24},{9,... | collective-permute-start | bytes 29712392 | tf_op jit(solution)/shard_map/ppermute | solution.py:33
  229.1 689.9 %all-gather.17.cloned.1.call-start = ((), (), s32[]{:S(2)}) async-start(), calls=%async_computation.6 | async-start | bytes 7864320 | tf_op jit(solution)/shard_map/all_gather | solution.py:48
  700.4 77.6 %copy-start.57 = (f32[1536]{0:T(1024)}, f32[1536]{0:T(1024)S(1)}, u32[]{:S(2)}) copy-start(f32[1536]{0:T(1024)S(1)} %convert_element_type.93) | copy-start | bytes 18436
  741.8 88.0 %copy-start.75 = (f32[3328]{0:T(1024)}, f32[3328]{0:T(1024)S(1)}, u32[]{:S(2)}) copy-start(f32[3328]{0:T(1024)S(1)} %get-tuple-element.1307) | copy-start | bytes 39940
  742.8 35.2 %copy-start.109 = (f32[256]{0:T(256)}, f32[256]{0:T(256)S(1)}, u32[]{:S(2)}) copy-start(f32[256]{0:T(256)S(1)} %fusion.250) | copy-start | bytes 3076
  742.8 18.4 copy-start.107
  801.9 75.2 %copy-start.48 = (f32[48,2,128]{0,2,1:T(8,128)}, f32[48,2,128]{0,2,1:T(8,128)S(1)}, u32[]{:S(2)}) copy-start(f32[48,2,128]{0,2,1:T(8,128)S(1)} %copy.315) | copy-start | bytes 147460
  803.0 26.8 %collective-permute-start.5 = (f32[3,3328]{1,0:T(4,128)}, f32[3,3328]{1,0:T(4,128)}, u32[]{:S(2)}, u32[]{:S(2)}) collective-permute-start(f32[3,3328]{1,0:T(4,128)} %copy.298), channel_id=1, source_target_pairs={{0,1},{1,2},{2,3},{4,5},{5,6},{6,7},{8,9},{9,10},{10,11},{12,13},{... | collective-permute-start | bytes 119816 | tf_op jit(solution)/shard_map/ppermute | solution.py:43
  807.0 22.8 %collective-permute-start.6 = (f32[3,3328]{1,0:T(4,128)}, f32[3,3328]{1,0:T(4,128)}, u32[]{:S(2)}, u32[]{:S(2)}) collective-permute-start(f32[3,3328]{1,0:T(4,128)} %copy.311), channel_id=1, source_target_pairs={{0,1},{1,2},{2,3},{4,5},{5,6},{6,7},{8,9},{9,10},{10,11},{12,13},{... | collective-permute-start | bytes 119816 | tf_op jit(solution)/shard_map/ppermute | solution.py:43
  853.3 105.3 %all-gather.15.cloned.1.call-start = ((), (), s32[]{:S(2)}) async-start(), calls=%async_computation.5 | async-start | bytes 7864320 | tf_op jit(solution)/shard_map/all_gather | solution.py:48
  854.4 27.3 %copy-start.46 = (f32[48,2,128]{0,2,1:T(8,128)}, f32[48,2,128]{0,2,1:T(8,128)S(1)}, u32[]{:S(2)}) copy-start(f32[48,2,128]{0,2,1:T(8,128)S(1)} %copy.302) | copy-start | bytes 147460
  867.6 274.0 %all-gather.21.cloned.1.call-start = ((), (), s32[]{:S(2)}) async-start(), calls=%async_computation.8 | async-start | bytes 7864320 | tf_op jit(solution)/shard_map/all_gather | solution.py:48
  908.5 162.9 %copy-start.70 = (f32[256,256]{1,0:T(8,128)}, f32[256,256]{1,0:T(8,128)S(1)}, u32[]{:S(2)}) copy-start(f32[256,256]{1,0:T(8,128)S(1)} %fusion.234) | copy-start | bytes 786436
  926.4 23.2 %copy-start.2 = (f32[48,64,128]{2,1,0:T(8,128)}, f32[48,64,128]{2,1,0:T(8,128)S(1)}, u32[]{:S(2)}) copy-start(f32[48,64,128]{2,1,0:T(8,128)S(1)} %get-tuple-element.1188) | copy-start | bytes 4718596
  926.4 23.2 %copy-start.127 = (f32[4,48]{1,0:T(4,128)}, f32[4,48]{1,0:T(4,128)S(1)}, u32[]{:S(2)}) copy-start(f32[4,48]{1,0:T(4,128)S(1)} %get-tuple-element.1733) | copy-start | bytes 2308
  930.6 19.0 copy-start.36
  958.6 53.0 %copy-start.111 = (f32[256]{0:T(256)}, f32[256]{0:T(256)S(1)}, u32[]{:S(2)}) copy-start(f32[256]{0:T(256)S(1)} %fusion.251) | copy-start | bytes 3076
  969.7 19.2 copy-start.37
  998.0 135.7 %copy-start.113 = (f32[256]{0:T(256)}, f32[256]{0:T(256)S(1)}, u32[]{:S(2)}) copy-start(f32[256]{0:T(256)S(1)} %fusion.249) | copy-start | bytes 3076
  998.0 13.6 copy-start.19
  1036.4 134.1 %all-gather.19.cloned.1.call-start = ((), (), s32[]{:S(2)}) async-start(), calls=%async_computation.7 | async-start | bytes 7864320 | tf_op jit(solution)/shard_map/all_gather | solution.py:48
  1046.5 469.7 %all-reduce.43.cloned.1.call-start = ((), (), s32[]{:S(2)}) async-start(), calls=%async_computation.9 | async-start | bytes 183296
  1058.3 13.2 copy-start.72
  1058.3 13.2 copy-start.85
  1058.3 13.3 copy-start.90
  1058.3 13.3 copy-start.93
  1058.3 13.3 copy-start.96
  1058.3 13.3 copy-start.99
  1141.6 15.4 copy-start.67
  1248.9 16.8 copy-start.33
  1297.0 51.3 %copy-start.34 = (f32[256,3328]{1,0:T(8,128)S(1)}, f32[256,3328]{1,0:T(8,128)}, u32[]{:S(2)}) copy-start(f32[256,3328]{1,0:T(8,128)} %split.20) | copy-start | bytes 10223620
  1338.5 20.1 collective-permute-start.8
  1339.8 33.5 %collective-permute-start.7 = (bf16[3,3328]{1,0:T(4,128)(2,1)}, bf16[3,3328]{1,0:T(4,128)(2,1)}, u32[]{:S(2)}, u32[]{:S(2)}) collective-permute-start(bf16[3,3328]{1,0:T(4,128)(2,1)} %split.25), channel_id=1, source_target_pairs={{1,0},{2,1},{3,2},{5,4},{6,5},{7,6},{9,8},{10,9},{11,10},{13,12},{... | collective-permute-start | bytes 59912 | tf_op jit(solution)/shard_map/ppermute | solution.py:43
  1360.9 15.2 copy-start.58
  1360.9 15.2 copy-start.108
  1360.9 15.2 copy-start.110
  1376.1 14.3 copy-start.18
  1376.1 14.3 copy-start.112
  1390.4 340.6 %reduce-scatter.6.cloned.1.call-start = ((), (), s32[]{:S(2)}) async-start(), calls=%async_computation.4 | async-start | bytes 19464192 | tf_op jit(solution)/shard_map/reduce_scatter | solution.py:152
  1402.8 697.9 %reduce-scatter.4.cloned.1.call-start = ((), (), s32[]{:S(2)}) async-start(), calls=%async_computation.3 | async-start | bytes 41361408 | tf_op jit(solution)/shard_map/reduce_scatter | solution.py:147
  (111 other events, 610.7 us)
Sparse Core Ops, SparseCore 0:
  229.2 487.9 all-gather.12
  853.4 42.2 all-gather.16
  897.8 46.3 all-gather.14
  1036.5 42.4 all-gather.20
  1080.5 46.3 all-gather.18
  1390.5 125.6 all-reduce.42
  1523.2 207.7 reduce-scatter.5
  1737.9 362.6 reduce-scatter.3
